TPU v7x, 32 devices: a whole 2x2x4 slice. The times are simulated.
32 devices in a mesh: seq: 4 (over y, x), exp: 8 (over z, core).
Axes of the slice: x: 2, y: 2, z: 4, core: 2. Of those that a mesh axis runs over, the one named last changes fastest.
Arguments:
- queries: bfloat16 [4096, 3072], P(('seq', 'exp')), may hold values from -123 to 123
- keys: bfloat16 [4096, 512], P(('seq', 'exp')), may hold values from -6 to 6
- values: bfloat16 [4096, 512], P(('seq', 'exp')), may hold values from -9 to 9
- residual: bfloat16 [4096, 6144], P(('seq', 'exp')), may hold values from -51 to 51
- proj_weight: bfloat16 [3072, 6144], P('seq', 'exp'), may hold values from -0.109375 to 0.109375
- norm_gain: bfloat16 [6144], replicated, may hold values from 0.099609375 to 1.8984375
- router: bfloat16 [6144, 8], replicated, may hold values from -0.078125 to 0.078125
- expert_ids: int32 [4096, 2], P(('seq', 'exp')), may hold values from 0 to 7, all different within a row; in each aligned block of 128 rows (0 to 127, 128 to 255, ...) at most 33 rows name the same one
- u_gate_up: bfloat16 [8, 6144, 1024], P('exp'), may hold values from -0.078125 to 0.078125
- v_gate_up: bfloat16 [8, 2, 512, 8192], P('exp'), may hold values from -0.25 to 0.25
- u_down: bfloat16 [8, 8192, 512], P('exp'), may hold values from -0.0625 to 0.0625
- v_down: bfloat16 [8, 512, 6144], P('exp'), may hold values from -0.25 to 0.25
Outputs:
- layer_out: bfloat16 [4096, 6144], P(('seq', 'exp'))
Inputs may be any that keep to these rules, and one draw needn't show every extreme that they name: `expert_ids`: the two experts of a token differ. Among the tokens of one device no expert is named more than 33 times, and in some devices' tokens some expert is named exactly 33 times.
All inputs are finite; a program needn't handle non-finite values.
Results may differ from a plain program's by a relative error of at most 0.02.
Values may be sent and summed in bfloat16 or wider, within the bound.
A program may use at most 192 MiB of HBM per device.

v0:
```python
import jax
import jax.numpy as jnp
from jax import lax
from jax.sharding import PartitionSpec as P

D = 6144
HEADS = 24
KV_HEADS = 4
HEAD_DIM = 128
GROUP_HEADS = 3
EXPERTS = 8
RANK = 512
TOK_DEV = 128
CAP = 33
EPS = 1e-05


def swapped(x, axis, distance):
    return lax.ppermute(x, axis, [(i, i ^ 1 << distance) for i in range(lax.axis_size(axis))])


def passed_along(value, axis, steps):
    count = lax.axis_size(axis)
    pairs = [(source, (source + steps) % count) for source in range(count)]
    return lax.ppermute(value, axis, pairs)


def attend(current, query_rows, key_rows, value_rows, allowed):
    row_max, row_sum, weighted = current
    scores = jnp.einsum("qhd,kd->qhk", query_rows, key_rows, preferred_element_type=jnp.float32)
    scores = scores * HEAD_DIM ** (-0.5)
    if allowed is not None:
        scores = jnp.where(allowed[:, None, :], scores, -jnp.inf)
    new_max = jnp.maximum(row_max, jnp.max(scores, axis=-1))
    fading = jnp.exp(row_max - new_max)
    exp_terms = jnp.exp(scores - new_max[..., None])
    row_sum = row_sum * fading + jnp.sum(exp_terms, axis=-1)
    update = jnp.einsum(
        "qhk,kd->qhd",
        exp_terms.astype(jnp.bfloat16),
        value_rows,
        preferred_element_type=jnp.float32,
    )
    weighted = weighted * fading[..., None] + update
    return (new_max, row_sum, weighted)


def fresh_states(count_rows):
    query_step = min(512, count_rows)
    states = [
        (
            jnp.full((query_step, GROUP_HEADS), -1e30, jnp.float32),
            jnp.zeros((query_step, GROUP_HEADS), jnp.float32),
            jnp.zeros((query_step, GROUP_HEADS, HEAD_DIM), jnp.float32),
        )
    ]
    return states


def attend_all(states, query_rows, query_pos, key_rows, value_rows, key_pos, mode):
    current = states[0]
    if mode == "open":
        current = attend(current, query_rows, key_rows, value_rows, None)
    else:
        allowed = key_pos[None, :] <= query_pos[:, None]
        current = attend(current, query_rows, key_rows, value_rows, allowed)
    updated = [current]
    return updated


def pick_states(stacked, which):
    return [
        tuple((lax.dynamic_index_in_dim(member, which, 0, keepdims=False) for member in tile))
        for tile in stacked
    ]


def put_states(stacked, which, fresh):
    return [
        tuple(
            (
                lax.dynamic_update_index_in_dim(member, newer, which, 0)
                for member, newer in zip(tile, new_tile)
            )
        )
        for tile, new_tile in zip(stacked, fresh)
    ]


def finish(states):
    results = [weighted / row_sum[..., None] for row_max, row_sum, weighted in states]
    joined = results[0].astype(jnp.bfloat16)
    return joined.reshape(joined.shape[0], GROUP_HEADS * HEAD_DIM)


def per_device(
    queries,
    keys,
    values,
    residual,
    proj_weight,
    norm_gain,
    router,
    expert_ids,
    u_gate_up,
    v_gate_up,
    u_down,
    v_down,
):
    seq_count = lax.axis_size("seq")
    exp_count = lax.axis_size("exp")
    seq_index = lax.axis_index("seq")
    exp_index = lax.axis_index("exp")
    group_count = HEADS // GROUP_HEADS
    split_count = exp_count // group_count
    group_width = GROUP_HEADS * HEAD_DIM
    token_rows = TOK_DEV // split_count
    block_len = TOK_DEV * exp_count
    query_count = exp_count * token_rows
    per_kv = group_count // KV_HEADS
    half_index = exp_index // group_count
    query_send = queries.reshape(token_rows, exp_count, group_width)
    kv_shape = (TOK_DEV, split_count, KV_HEADS, per_kv, HEAD_DIM)
    key_send = jnp.broadcast_to(keys.reshape(TOK_DEV, 1, KV_HEADS, 1, HEAD_DIM), kv_shape).reshape(
        TOK_DEV, exp_count, HEAD_DIM
    )
    value_send = jnp.broadcast_to(
        values.reshape(TOK_DEV, 1, KV_HEADS, 1, HEAD_DIM), kv_shape
    ).reshape(TOK_DEV, exp_count, HEAD_DIM)
    query_got, key_got, value_got = (
        lax.all_to_all(query_send, "exp", split_axis=1, concat_axis=0, tiled=True),
        lax.all_to_all(key_send, "exp", split_axis=1, concat_axis=0, tiled=True),
        lax.all_to_all(value_send, "exp", split_axis=1, concat_axis=0, tiled=True),
    )
    query_local = query_got.reshape(query_count, GROUP_HEADS, HEAD_DIM)
    key_local = key_got.reshape(block_len, HEAD_DIM)
    value_local = value_got.reshape(block_len, HEAD_DIM)
    row_ids = jnp.arange(query_count, dtype=jnp.int32)
    in_block = row_ids // token_rows * TOK_DEV + row_ids % token_rows * split_count + half_index
    key_offsets = jnp.arange(block_len, dtype=jnp.int32)
    half_q = query_count // 2
    half_k = block_len // 2
    query_near = query_local[:half_q]
    query_far = query_local[half_q:]
    key_far = key_local[half_k:]
    value_far = value_local[half_k:]
    for bit_index in range(seq_count.bit_length() - 1):
        query_far, key_far, value_far = swapped((query_far, key_far, value_far), "seq", bit_index)
    mirror_index = seq_count - 1 - seq_index
    near_pos = seq_index * block_len + in_block[:half_q]
    far_pos = mirror_index * block_len + in_block[half_q:]
    query_pair = jnp.stack([query_near, query_far])
    pair_states = [
        tuple((jnp.stack([member, member]) for member in tile)) for tile in fresh_states(half_q)
    ]
    held_blocks = (key_local[:half_k], value_local[:half_k], key_far, value_far)
    for step_index in range(seq_count):
        if step_index + 1 < seq_count:
            arrived = passed_along(
                (held_blocks[0], held_blocks[1], held_blocks[2], held_blocks[3]), "seq", 1
            )
        source = (seq_index - step_index) % seq_count
        low_keys, low_values, high_keys, high_values = held_blocks
        if step_index == 0:
            low_pos = source * block_len + key_offsets[:half_k]
            high_pos = (seq_count - 1 - source) * block_len + half_k + key_offsets[:half_k]
            near_now = pick_states(pair_states, 0)
            near_now = attend_all(
                near_now, query_near, near_pos, low_keys, low_values, low_pos, "masked"
            )
            pair_states = put_states(pair_states, 0, near_now)
            far_now = pick_states(pair_states, 1)
            far_now = attend_all(
                far_now, query_far, far_pos, high_keys, high_values, high_pos, "masked"
            )
            pair_states = put_states(pair_states, 1, far_now)
        else:
            first_low = source <= seq_index
            first_slot = jnp.where(first_low, 0, 1).astype(jnp.int32)
            key_pick = jnp.where(first_low, low_keys, high_keys)
            value_pick = jnp.where(first_low, low_values, high_values)
            query_pick = lax.dynamic_index_in_dim(query_pair, first_slot, 0, keepdims=False)
            picked_states = attend_all(
                pick_states(pair_states, first_slot),
                query_pick,
                None,
                key_pick,
                value_pick,
                None,
                "open",
            )
            pair_states = put_states(pair_states, first_slot, picked_states)
        second_high = source >= seq_count - seq_index
        second_slot = jnp.where(second_high, 0, 1).astype(jnp.int32)
        key_pick = jnp.where(second_high, high_keys, low_keys)
        value_pick = jnp.where(second_high, high_values, low_values)
        query_pick = lax.dynamic_index_in_dim(query_pair, second_slot, 0, keepdims=False)
        picked_states = attend_all(
            pick_states(pair_states, second_slot),
            query_pick,
            None,
            key_pick,
            value_pick,
            None,
            "open",
        )
        pair_states = put_states(pair_states, second_slot, picked_states)
        if step_index + 1 < seq_count:
            held_blocks = arrived
    attended_near = finish(pick_states(pair_states, 0))
    attended_far = finish(pick_states(pair_states, 1))
    for bit_index in range(seq_count.bit_length() - 1):
        attended_far = swapped(attended_far, "seq", bit_index)
    attended = jnp.concatenate([attended_near, attended_far], axis=0)
    weight_rows = lax.all_gather(proj_weight, "seq", axis=0, tiled=True)
    column_count = weight_rows.shape[1]
    blank_sum = jnp.zeros((exp_count, token_rows, split_count, column_count), jnp.float32)
    carried = blank_sum
    shard_piece = lax.all_gather(attended, "exp", axis=0, tiled=True)
    start_row = jnp.int32(0)
    shard_total = shard_piece.shape[0] // query_count
    for shard_index in range(shard_total):
        device_id = start_row // query_count + shard_index
        group_id = device_id % group_count
        half_id = device_id // group_count
        weight_slice = lax.dynamic_slice_in_dim(weight_rows, group_id * group_width, group_width, 0)
        rows_now = shard_piece[shard_index * query_count : (shard_index + 1) * query_count]
        product = jnp.dot(rows_now, weight_slice, preferred_element_type=jnp.float32)
        product = product.reshape(exp_count, token_rows, 1, column_count)
        corner = (0, 0, half_id, 0)
        present = lax.dynamic_slice(carried, corner, (exp_count, token_rows, 1, column_count))
        carried = lax.dynamic_update_slice(carried, present + product, corner)
    projected = carried
    projected = projected.reshape(block_len, column_count)
    attn_block = projected.astype(jnp.bfloat16)
    attn_update = lax.all_to_all(attn_block, "exp", split_axis=0, concat_axis=1, tiled=True)
    stream = residual.astype(jnp.float32) + attn_update.astype(jnp.float32)
    mean_sq = jnp.mean(stream * stream, axis=-1, keepdims=True)
    normed = (stream * lax.rsqrt(mean_sq + EPS) * norm_gain.astype(jnp.float32)).astype(
        jnp.bfloat16
    )
    logits = jnp.dot(normed, router, preferred_element_type=jnp.float32)
    expert_range = jnp.arange(EXPERTS, dtype=jnp.int32)
    picked = (expert_ids[:, :, None] == expert_range[None, None, :]).astype(jnp.float32)
    chosen = jnp.sum(picked * logits[:, None, :], axis=-1)
    mix_first = jax.nn.sigmoid(chosen[:, 0] - chosen[:, 1])
    mix_second = jax.nn.sigmoid(chosen[:, 1] - chosen[:, 0])
    piece_count = exp_count // EXPERTS
    piece_width = D // piece_count
    flat_ids = expert_ids.reshape(TOK_DEV * 2)
    member = (flat_ids[:, None] == expert_range[None, :]).astype(jnp.int32)
    slot_of = jnp.sum((jnp.cumsum(member, axis=0) - 1) * member, axis=1)
    token_of = jnp.arange(TOK_DEV * 2, dtype=jnp.int32) // 2
    slot_range = jnp.arange(CAP, dtype=jnp.int32)
    filled = member[:, :, None] * (slot_of[:, None, None] == slot_range[None, None, :]).astype(
        jnp.int32
    )
    source_token = jnp.sum(filled * token_of[:, None, None], axis=0)
    occupied = jnp.sum(filled, axis=0)
    piece_range = jnp.arange(piece_count, dtype=jnp.int32)
    take_index = source_token[:, None, :] * piece_count + piece_range[None, :, None]
    normed_rows = normed.reshape(TOK_DEV * piece_count, piece_width)
    send_rows = jnp.take(normed_rows, take_index, axis=0) * occupied[:, None, :, None].astype(
        jnp.bfloat16
    )
    send_rows = send_rows.reshape(exp_count, CAP, piece_width)
    dispatched = lax.all_to_all(send_rows, "exp", split_axis=0, concat_axis=0, tiled=True)
    expert_rows = dispatched.reshape(exp_count * CAP, piece_width)
    rank_sum = jnp.dot(expert_rows, u_gate_up[0], preferred_element_type=jnp.float32)
    for bit_index in range(piece_count.bit_length() - 1):
        rank_sum = rank_sum + swapped(rank_sum.astype(jnp.bfloat16), "exp", bit_index).astype(
            rank_sum.dtype
        )
    rank_in = rank_sum.astype(jnp.bfloat16)
    gate_part = jnp.dot(rank_in[:, :RANK], v_gate_up[0, 0], preferred_element_type=jnp.float32)
    up_part = jnp.dot(rank_in[:, RANK:], v_gate_up[0, 1], preferred_element_type=jnp.float32)
    hidden = (jax.nn.silu(gate_part) * up_part).astype(jnp.bfloat16)
    down_sum = jnp.dot(hidden, u_down[0], preferred_element_type=jnp.float32)
    for bit_index in range(piece_count.bit_length() - 1):
        down_sum = down_sum + swapped(down_sum.astype(jnp.bfloat16), "exp", bit_index).astype(
            down_sum.dtype
        )
    expert_out = jnp.dot(
        down_sum.astype(jnp.bfloat16), v_down[0], preferred_element_type=jnp.float32
    ).astype(jnp.bfloat16)
    returned = lax.all_to_all(
        expert_out.reshape(exp_count, CAP, piece_width),
        "exp",
        split_axis=0,
        concat_axis=0,
        tiled=True,
    )
    returned_rows = returned.reshape(exp_count * CAP, piece_width)
    slot_pairs = slot_of.reshape(TOK_DEV, 2)
    fetch_index = (
        expert_ids[:, :, None] * piece_count + piece_range[None, None, :]
    ) * CAP + slot_pairs[:, :, None]
    fetched = jnp.take(returned_rows, fetch_index, axis=0).astype(jnp.float32)
    fetched = fetched.reshape(TOK_DEV, 2, D)
    mixture = mix_first[:, None] * fetched[:, 0] + mix_second[:, None] * fetched[:, 1]
    return (stream + mixture).astype(jnp.bfloat16)


def solution(mesh):
    in_specs = (
        P(("seq", "exp"), None),
        P(("seq", "exp"), None),
        P(("seq", "exp"), None),
        P(("seq", "exp"), None),
        P("seq", "exp"),
        P(),
        P(),
        P(("seq", "exp"), None),
        P("exp", None, None),
        P("exp", None, None, None),
        P("exp", None, None),
        P("exp", None, None),
    )
    out_specs = P(("seq", "exp"), None)
    return jax.shard_map(
        per_device, mesh=mesh, in_specs=in_specs, out_specs=out_specs, check_vma=False
    )
```

profile of v0, /device:TPU:0, one launch (start us, length us, event | category | flops | bytes accessed | tf_op | source)
XLA Modules:
  0.0 555.5 jit_solution(10118629330337509046)
XLA Ops:
  8.2 6.4 %all-to-all-start.1 = ((bf16[128,8,128]{2,0,1:T(8,128)(2,1)}), bf16[128,8,128]{2,0,1:T(8,128)(2,1)S(1)}, u32[]{:S(2)}, u32[]{:S(2)}) async-start(bf16[128,8,128]{2,0,1:T(8,128)(2,1)} %bitcast.3), calls=%async_computation.1 | async-start | bytes 524288 | tf_op jit(solution)/shard_map/all_to_all | solution.py:132
  15.5 8.8 %all-to-all-done.1 = bf16[128,8,128]{2,0,1:T(8,128)(2,1)S(1)} async-done(((bf16[128,8,128]{2,0,1:T(8,128)(2,1)}), bf16[128,8,128]{2,0,1:T(8,128)(2,1)S(1)}, u32[]{:S(2)}, u32[]{:S(2)}) %all-to-all-start.1) | async-done | bytes 262176 | tf_op jit(solution)/shard_map/all_to_all | solution.py:132
  25.0 3.4 all-to-all-start.2
  28.4 2.3 copy.180
  30.7 7.3 %all-to-all-done.2 = bf16[128,8,128]{2,0,1:T(8,128)(2,1)S(1)} async-done(((bf16[128,8,128]{2,0,1:T(8,128)(2,1)}), bf16[128,8,128]{2,0,1:T(8,128)(2,1)S(1)}, u32[]{:S(2)}, u32[]{:S(2)}) %all-to-all-start.2) | async-done | bytes 262176 | tf_op jit(solution)/shard_map/all_to_all | solution.py:133
  38.0 3.5 all-to-all-start
  41.7 1.6 collective-permute-start.2
  44.1 4.0 collective-permute-done.2
  48.1 1.5 collective-permute-start.3
  50.3 1.5 collective-permute-start.5
  55.3 9.3 %collective-permute-done.5 = bf16[512,128]{1,0:T(8,128)(2,1)S(1)} collective-permute-done((bf16[512,128]{1,0:T(8,128)(2,1)S(1)}, bf16[512,128]{1,0:T(8,128)(2,1)S(1)}, u32[]{:S(2)}, u32[]{:S(2)}) %collective-permute-start.5) | collective-permute-done | bytes 131104 | tf_op jit(solution)/shard_map/ppermute | solution.py:19
  64.9 4.6 collective-permute-start.10
  69.5 2.7 collective-permute-done.7
  73.5 4.3 collective-permute-done.9
  79.4 3.6 collective-permute-done.10
  83.3 2.5 collective-permute-done.12
  86.1 2.5 collective-permute-done.11
  88.9 2.5 collective-permute-done.13
  97.1 11.4 %collective-permute-done = bf16[512,3,128]{2,0,1:T(8,128)(2,1)} collective-permute-done((bf16[512,3,128]{2,0,1:T(8,128)(2,1)}, bf16[512,3,128]{2,0,1:T(8,128)(2,1)}, u32[]{:S(2)}, u32[]{:S(2)}) %collective-permute-start) | collective-permute-done | bytes 393248 | tf_op jit(solution)/shard_map/ppermute | solution.py:19
  108.5 1.5 collective-permute-start.1
  110.4 2.8 fusion.149
  113.3 15.1 %collective-permute-done.1 = bf16[512,3,128]{2,0,1:T(8,128)(2,1)S(1)} collective-permute-done((bf16[512,3,128]{2,0,1:T(8,128)(2,1)}, bf16[512,3,128]{2,0,1:T(8,128)(2,1)S(1)}, u32[]{:S(2)}, u32[]{:S(2)}) %collective-permute-start.1) | collective-permute-done | bytes 393248 | tf_op jit(solution)/shard_map/ppermute | solution.py:19
  147.0 7.8 %collective-permute-done.18 = bf16[512,384]{0,1:T(8,128)(2,1)S(1)} collective-permute-done((bf16[512,384]{0,1:T(8,128)(2,1)S(1)}, bf16[512,384]{0,1:T(8,128)(2,1)S(1)}, u32[]{:S(2)}, u32[]{:S(2)}) %collective-permute-start.18) | collective-permute-done | bytes 393248 | tf_op jit(solution)/shard_map/ppermute | solution.py:19
  155.7 7.4 %collective-permute-done.19 = bf16[512,384]{0,1:T(8,128)(2,1)S(1)} collective-permute-done((bf16[512,384]{0,1:T(8,128)(2,1)S(1)}, bf16[512,384]{0,1:T(8,128)(2,1)S(1)}, u32[]{:S(2)}, u32[]{:S(2)}) %collective-permute-start.19) | collective-permute-done | bytes 393248 | tf_op jit(solution)/shard_map/ppermute | solution.py:19
  164.1 63.2 %all-gather.3.cloned.1.call-done = bf16[8192,384]{0,1:T(8,128)(2,1)} async-done(((bf16[1024,384]{0,1:T(8,128)(2,1)}), bf16[8192,384]{0,1:T(8,128)(2,1)}) %all-gather.3.cloned.1.call-update) | async-done | bytes 6291472 | tf_op jit(solution)/shard_map/all_gather | solution.py:219
  227.3 2.5 fusion.167
  229.8 2.5 fusion.169
  232.2 2.1 fusion.171
  238.9 3.8 add_convert_fusion
  242.7 3.7 all-to-all-start.3
  249.4 34.8 %all-to-all-done.3 = bf16[8,128,768]{2,1,0:T(8,128)(2,1)S(1)} async-done(((bf16[8,128,768]{2,1,0:T(8,128)(2,1)}), bf16[8,128,768]{2,1,0:T(8,128)(2,1)S(1)}, u32[]{:S(2)}, u32[]{:S(2)}) %all-to-all-start.3) | async-done | bytes 1572896 | tf_op jit(solution)/shard_map/all_to_all | solution.py:236
  287.1 5.0 gather_fusion
  292.2 4.9 gather.13
  297.1 2.5 select_multiply_fusion
  299.7 91.9 %all_to_all.68 = bf16[8,33,6144]{2,1,0:T(8,128)(2,1)} all-to-all(bf16[8,33,6144]{2,1,0:T(8,128)(2,1)S(1)} %select_multiply_fusion), channel_id=1, replica_groups=mesh['seq'=4,'exp'=8] {'exp'}, dimensions={0} | all-to-all | bytes 6488064 | tf_op jit(solution)/shard_map/all_to_all | solution.py:267
  391.5 5.0 reshape.493
  396.5 9.1 %fusion.80 = bf16[264,1024]{1,0:T(8,128)(2,1)S(1)} fusion(bf16[264,6144]{1,0:T(8,128)(2,1)} %reshape.493, bf16[1,6144,1024]{2,1,0:T(8,128)(2,1)} %param.20), kind=kOutput, calls=%fused_computation.117 | convolution fusion | flops 3322159104 | bytes 16367616 | tf_op jit(solution)/shard_map/dot_general | solution.py:269
  405.6 9.1 %fusion.6 = f32[264,8192]{1,0:T(8,128)} fusion(bf16[1,2,512,8192]{3,2,1,0:T(8,128)(2,1)} %param.21, bf16[264,1024]{1,0:T(8,128)(2,1)S(1)} %fusion.80), kind=kOutput, calls=%fused_computation.9 | convolution fusion | flops 2214592512 | bytes 17309696 | tf_op jit(solution)/shard_map/dot_general | solution.py:275
  414.8 11.2 %fusion.158 = bf16[264,512]{1,0:T(8,128)(2,1)S(1)} fusion(bf16[1,8192,512]{2,1,0:T(8,128)(2,1)} %param.22, f32[264,8192]{1,0:T(8,128)} %fusion.6, bf16[1,2,512,8192]{3,2,1,0:T(8,128)(2,1)} %param.21, bf16[264,1024]{1,0:T(8,128)(2,1)S(1)} %fusion.80), kind=kOutput, calls=%fused_computation.143 | convolution fusion | flops 4442296320 | bytes 25968640 | tf_op jit(solution)/shard_map/dot_general | solution.py:278
  425.9 6.4 %convolution_convert_fusion = bf16[264,6144]{1,0:T(8,128)(2,1)} fusion(bf16[264,512]{1,0:T(8,128)(2,1)S(1)} %fusion.158, bf16[1,512,6144]{2,1,0:T(8,128)(2,1)} %param.23), kind=kOutput, calls=%fused_computation.13 | convolution fusion | flops 1662566400 | bytes 9805824 | tf_op jit(solution)/shard_map/dot_general | solution.py:283
  432.3 4.9 reshape.494
  437.2 4.9 all-to-all-start.5
  443.2 87.3 %all-to-all-done.5 = bf16[8,33,6144]{2,1,0:T(8,128)(2,1)} async-done(((bf16[8,33,6144]{2,1,0:T(8,128)(2,1)}), bf16[8,33,6144]{2,1,0:T(8,128)(2,1)}, u32[]{:S(2)}, u32[]{:S(2)}) %all-to-all-start.5) | async-done | bytes 3244064 | tf_op jit(solution)/shard_map/all_to_all | solution.py:286
  530.5 3.3 reshape.495
  533.8 4.1 gather_fusion.1
  537.8 5.9 %gather.15 = bf16[128,2,6144]{2,1,0:T(2,128)(2,1)S(1)} reshape(bf16[256,6144]{1,0:T(8,128)(2,1)} %gather_fusion.1) | data formatting | bytes 6291456 | tf_op jit(solution)/shard_map/jit(_take)/gather | solution.py:298
  543.8 2.0 fusion.19
  546.1 2.3 fusion.17
  (181 shorter events, 50.2 us)
Async XLA Ops:
  6.5 0.9 copy-start
  8.2 16.1 %all-to-all-start.1 = ((bf16[128,8,128]{2,0,1:T(8,128)(2,1)}), bf16[128,8,128]{2,0,1:T(8,128)(2,1)S(1)}, u32[]{:S(2)}, u32[]{:S(2)}) async-start(bf16[128,8,128]{2,0,1:T(8,128)(2,1)} %bitcast.3), calls=%async_computation.1 | async-start | bytes 524288 | tf_op jit(solution)/shard_map/all_to_all | solution.py:132
  25.0 13.1 %all-to-all-start.2 = ((bf16[128,8,128]{2,0,1:T(8,128)(2,1)}), bf16[128,8,128]{2,0,1:T(8,128)(2,1)S(1)}, u32[]{:S(2)}, u32[]{:S(2)}) async-start(bf16[128,8,128]{2,0,1:T(8,128)(2,1)} %bitcast.8), calls=%async_computation.2 | async-start | bytes 524288 | tf_op jit(solution)/shard_map/all_to_all | solution.py:133
  38.0 53.9 %all-to-all-start = ((bf16[128,8,384]{0,2,1:T(8,128)(2,1)}), bf16[128,8,384]{0,2,1:T(8,128)(2,1)S(1)}, u32[]{:S(2)}, u32[]{:S(2)}) async-start(bf16[128,8,384]{0,2,1:T(8,128)(2,1)} %bitcast), calls=%async_computation | async-start | bytes 1572864 | tf_op jit(solution)/shard_map/all_to_all | solution.py:131
  41.6 122.5 %all-gather.5.cloned.1.call-start = ((), (), s32[]{:S(2)}) async-start(), calls=%async_computation.7 | async-start | bytes 5898240 | tf_op jit(solution)/shard_map/all_gather | solution.py:215
  41.7 6.4 %collective-permute-start.2 = (bf16[512,128]{1,0:T(8,128)(2,1)S(1)}, bf16[512,128]{1,0:T(8,128)(2,1)S(1)}, u32[]{:S(2)}, u32[]{:S(2)}) collective-permute-start(bf16[512,128]{1,0:T(8,128)(2,1)S(1)} %bitcast.406), channel_id=1, source_target_pairs={{0,8},{8,0},{16,24},{24,16},{1,9},{9,1},{17,25},{25,17},{2,10},{10... | collective-permute-start | bytes 393224 | tf_op jit(solution)/shard_map/ppermute | solution.py:19
  43.3 26.2 %copy-start.9 = (bf16[4,128,1,128]{3,1,0,2:T(8,128)(2,1)}, bf16[4,128,1,128]{3,1,0,2:T(8,128)(2,1)S(1)}, u32[]{:S(2)}) copy-start(bf16[4,128,1,128]{3,1,0,2:T(8,128)(2,1)S(1)} %get-tuple-element.29) | copy-start | bytes 393220
  43.3 7.0 %collective-permute-start.4 = (bf16[512,128]{1,0:T(8,128)(2,1)S(1)}, bf16[512,128]{1,0:T(8,128)(2,1)S(1)}, u32[]{:S(2)}, u32[]{:S(2)}) collective-permute-start(bf16[512,128]{1,0:T(8,128)(2,1)S(1)} %bitcast.407), channel_id=1, source_target_pairs={{0,8},{8,0},{16,24},{24,16},{1,9},{9,1},{17,25},{25,17},{2,10},{10... | collective-permute-start | bytes 393224 | tf_op jit(solution)/shard_map/ppermute | solution.py:19
  43.9 183.4 %all-gather.3.cloned.1.call-start = ((), (), s32[]{:S(2)}) async-start(), calls=%async_computation.6 | async-start | bytes 7077888 | tf_op jit(solution)/shard_map/all_gather | solution.py:219
  48.1 5.7 %collective-permute-start.3 = (bf16[512,128]{1,0:T(8,128)(2,1)S(1)}, bf16[512,128]{1,0:T(8,128)(2,1)S(1)}, u32[]{:S(2)}, u32[]{:S(2)}) collective-permute-start(bf16[512,128]{1,0:T(8,128)(2,1)S(1)} %collective-permute-done.2), channel_id=1, source_target_pairs={{0,16},{8,24},{16,0},{24,8},{1,17},{9,25},{17,1},{25,9},{2,18},{10... | collective-permute-start | bytes 393224 | tf_op jit(solution)/shard_map/ppermute | solution.py:19
  50.3 14.3 %collective-permute-start.5 = (bf16[512,128]{1,0:T(8,128)(2,1)S(1)}, bf16[512,128]{1,0:T(8,128)(2,1)S(1)}, u32[]{:S(2)}, u32[]{:S(2)}) collective-permute-start(bf16[512,128]{1,0:T(8,128)(2,1)S(1)} %collective-permute-done.4), channel_id=1, source_target_pairs={{0,16},{8,24},{16,0},{24,8},{1,17},{9,25},{17,1},{25,9},{2,18},{10... | collective-permute-start | bytes 393224 | tf_op jit(solution)/shard_map/ppermute | solution.py:19
  51.8 13.0 %collective-permute-start.6 = (bf16[512,128]{1,0:T(8,128)(2,1)S(1)}, bf16[512,128]{1,0:T(8,128)(2,1)S(1)}, u32[]{:S(2)}, u32[]{:S(2)}) collective-permute-start(bf16[512,128]{1,0:T(8,128)(2,1)S(1)} %bitcast.398), channel_id=1, source_target_pairs={{0,8},{8,16},{16,24},{24,0},{1,9},{9,17},{17,25},{25,1},{2,10},{10... | collective-permute-start | bytes 393224 | tf_op jit(solution)/shard_map/ppermute | solution.py:25
  53.3 16.1 %collective-permute-start.8 = (bf16[512,128]{1,0:T(8,128)(2,1)S(1)}, bf16[512,128]{1,0:T(8,128)(2,1)S(1)}, u32[]{:S(2)}, u32[]{:S(2)}) collective-permute-start(bf16[512,128]{1,0:T(8,128)(2,1)S(1)} %bitcast.403), channel_id=1, source_target_pairs={{0,8},{8,16},{16,24},{24,0},{1,9},{9,17},{17,25},{25,1},{2,10},{10... | collective-permute-start | bytes 393224 | tf_op jit(solution)/shard_map/ppermute | solution.py:25
  53.8 18.4 %collective-permute-start.7 = (bf16[512,128]{1,0:T(8,128)(2,1)S(1)}, bf16[512,128]{1,0:T(8,128)(2,1)S(1)}, u32[]{:S(2)}, u32[]{:S(2)}) collective-permute-start(bf16[512,128]{1,0:T(8,128)(2,1)S(1)} %collective-permute-done.3), channel_id=1, source_target_pairs={{0,8},{8,16},{16,24},{24,0},{1,9},{9,17},{17,25},{25,1},{2,10},{10... | collective-permute-start | bytes 393224 | tf_op jit(solution)/shard_map/ppermute | solution.py:25
  64.6 21.5 %copy-start.11 = (bf16[512,128]{1,0:T(8,128)(2,1)}, bf16[512,128]{1,0:T(8,128)(2,1)S(1)}, u32[]{:S(2)}) copy-start(bf16[512,128]{1,0:T(8,128)(2,1)S(1)} %collective-permute-done.5) | copy-start | bytes 393220
  64.6 13.2 %collective-permute-start.9 = (bf16[512,128]{1,0:T(8,128)(2,1)S(1)}, bf16[512,128]{1,0:T(8,128)(2,1)S(1)}, u32[]{:S(2)}, u32[]{:S(2)}) collective-permute-start(bf16[512,128]{1,0:T(8,128)(2,1)S(1)} %collective-permute-done.5), channel_id=1, source_target_pairs={{0,8},{8,16},{16,24},{24,0},{1,9},{9,17},{17,25},{25,1},{2,10},{10... | collective-permute-start | bytes 393224 | tf_op jit(solution)/shard_map/ppermute | solution.py:25
  64.9 18.1 %collective-permute-start.10 = (bf16[512,128]{1,0:T(8,128)(2,1)S(1)}, bf16[512,128]{1,0:T(8,128)(2,1)S(1)}, u32[]{:S(2)}, u32[]{:S(2)}) collective-permute-start(bf16[512,128]{1,0:T(8,128)(2,1)S(1)} %collective-permute-done.6), channel_id=1, source_target_pairs={{0,8},{8,16},{16,24},{24,0},{1,9},{9,17},{17,25},{25,1},{2,10},{10... | collective-permute-start | bytes 393224 | tf_op jit(solution)/shard_map/ppermute | solution.py:25
  69.4 16.4 %collective-permute-start.12 = (bf16[512,128]{1,0:T(8,128)(2,1)S(1)}, bf16[512,128]{1,0:T(8,128)(2,1)S(1)}, u32[]{:S(2)}, u32[]{:S(2)}) collective-permute-start(bf16[512,128]{1,0:T(8,128)(2,1)S(1)} %collective-permute-done.8), channel_id=1, source_target_pairs={{0,8},{8,16},{16,24},{24,0},{1,9},{9,17},{17,25},{25,1},{2,10},{10... | collective-permute-start | bytes 393224 | tf_op jit(solution)/shard_map/ppermute | solution.py:25
  72.2 16.4 %collective-permute-start.11 = (bf16[512,128]{1,0:T(8,128)(2,1)S(1)}, bf16[512,128]{1,0:T(8,128)(2,1)S(1)}, u32[]{:S(2)}, u32[]{:S(2)}) collective-permute-start(bf16[512,128]{1,0:T(8,128)(2,1)S(1)} %collective-permute-done.7), channel_id=1, source_target_pairs={{0,8},{8,16},{16,24},{24,0},{1,9},{9,17},{17,25},{25,1},{2,10},{10... | collective-permute-start | bytes 393224 | tf_op jit(solution)/shard_map/ppermute | solution.py:25
  77.8 13.6 %collective-permute-start.13 = (bf16[512,128]{1,0:T(8,128)(2,1)S(1)}, bf16[512,128]{1,0:T(8,128)(2,1)S(1)}, u32[]{:S(2)}, u32[]{:S(2)}) collective-permute-start(bf16[512,128]{1,0:T(8,128)(2,1)S(1)} %collective-permute-done.9), channel_id=1, source_target_pairs={{0,8},{8,16},{16,24},{24,0},{1,9},{9,17},{17,25},{25,1},{2,10},{10... | collective-permute-start | bytes 393224 | tf_op jit(solution)/shard_map/ppermute | solution.py:25
  83.0 57.6 %collective-permute-start.14 = (bf16[512,128]{1,0:T(8,128)(2,1)S(1)}, bf16[512,128]{1,0:T(8,128)(2,1)S(1)}, u32[]{:S(2)}, u32[]{:S(2)}) collective-permute-start(bf16[512,128]{1,0:T(8,128)(2,1)S(1)} %collective-permute-done.10), channel_id=1, source_target_pairs={{0,8},{8,16},{16,24},{24,0},{1,9},{9,17},{17,25},{25,1},{2,10},{10... | collective-permute-start | bytes 393224 | tf_op jit(solution)/shard_map/ppermute | solution.py:25
  85.8 56.3 %collective-permute-start.16 = (bf16[512,128]{1,0:T(8,128)(2,1)S(1)}, bf16[512,128]{1,0:T(8,128)(2,1)S(1)}, u32[]{:S(2)}, u32[]{:S(2)}) collective-permute-start(bf16[512,128]{1,0:T(8,128)(2,1)S(1)} %collective-permute-done.12), channel_id=1, source_target_pairs={{0,8},{8,16},{16,24},{24,0},{1,9},{9,17},{17,25},{25,1},{2,10},{10... | collective-permute-start | bytes 393224 | tf_op jit(solution)/shard_map/ppermute | solution.py:25
  88.6 52.0 %collective-permute-start.15 = (bf16[512,128]{1,0:T(8,128)(2,1)S(1)}, bf16[512,128]{1,0:T(8,128)(2,1)S(1)}, u32[]{:S(2)}, u32[]{:S(2)}) collective-permute-start(bf16[512,128]{1,0:T(8,128)(2,1)S(1)} %collective-permute-done.11), channel_id=1, source_target_pairs={{0,8},{8,16},{16,24},{24,0},{1,9},{9,17},{17,25},{25,1},{2,10},{10... | collective-permute-start | bytes 393224 | tf_op jit(solution)/shard_map/ppermute | solution.py:25
  91.4 50.7 %collective-permute-start.17 = (bf16[512,128]{1,0:T(8,128)(2,1)S(1)}, bf16[512,128]{1,0:T(8,128)(2,1)S(1)}, u32[]{:S(2)}, u32[]{:S(2)}) collective-permute-start(bf16[512,128]{1,0:T(8,128)(2,1)S(1)} %collective-permute-done.13), channel_id=1, source_target_pairs={{0,8},{8,16},{16,24},{24,0},{1,9},{9,17},{17,25},{25,1},{2,10},{10... | collective-permute-start | bytes 393224 | tf_op jit(solution)/shard_map/ppermute | solution.py:25
  93.4 15.2 %collective-permute-start = (bf16[512,3,128]{2,0,1:T(8,128)(2,1)}, bf16[512,3,128]{2,0,1:T(8,128)(2,1)}, u32[]{:S(2)}, u32[]{:S(2)}) collective-permute-start(bf16[512,3,128]{2,0,1:T(8,128)(2,1)} %copy.188), channel_id=1, source_target_pairs={{0,8},{8,0},{16,24},{24,16},{1,9},{9,1},{17,25},{25,17},{2,10},{10... | collective-permute-start | bytes 1179656 | tf_op jit(solution)/shard_map/ppermute | solution.py:19
  95.5 1.6 copy-start.6
  96.2 12.3 %copy-start.14 = (f32[512,3]{0,1:T(4,128)}, f32[512,3]{0,1:T(4,128)S(1)}, u32[]{:S(2)}) copy-start(f32[512,3]{0,1:T(4,128)S(1)} %get-tuple-element.47) | copy-start | bytes 18436
  108.5 19.9 %collective-permute-start.1 = (bf16[512,3,128]{2,0,1:T(8,128)(2,1)}, bf16[512,3,128]{2,0,1:T(8,128)(2,1)S(1)}, u32[]{:S(2)}, u32[]{:S(2)}) collective-permute-start(bf16[512,3,128]{2,0,1:T(8,128)(2,1)} %collective-permute-done), channel_id=1, source_target_pairs={{0,16},{8,24},{16,0},{24,8},{1,17},{9,25},{17,1},{25,9},{2,18},{10... | collective-permute-start | bytes 1179656 | tf_op jit(solution)/shard_map/ppermute | solution.py:19
  129.8 1.3 copy-start.12
  131.1 1.1 copy-start.10
  145.7 9.1 %collective-permute-start.18 = (bf16[512,384]{0,1:T(8,128)(2,1)S(1)}, bf16[512,384]{0,1:T(8,128)(2,1)S(1)}, u32[]{:S(2)}, u32[]{:S(2)}) collective-permute-start(bf16[512,384]{0,1:T(8,128)(2,1)S(1)} %fusion.181), channel_id=1, source_target_pairs={{0,8},{8,0},{16,24},{24,16},{1,9},{9,1},{17,25},{25,17},{2,10},{10... | collective-permute-start | bytes 1179656 | tf_op jit(solution)/shard_map/ppermute | solution.py:19
  154.8 8.2 %collective-permute-start.19 = (bf16[512,384]{0,1:T(8,128)(2,1)S(1)}, bf16[512,384]{0,1:T(8,128)(2,1)S(1)}, u32[]{:S(2)}, u32[]{:S(2)}) collective-permute-start(bf16[512,384]{0,1:T(8,128)(2,1)S(1)} %collective-permute-done.18), channel_id=1, source_target_pairs={{0,16},{8,24},{16,0},{24,8},{1,17},{9,25},{17,1},{25,9},{2,18},{10... | collective-permute-start | bytes 1179656 | tf_op jit(solution)/shard_map/ppermute | solution.py:19
  227.3 5.0 copy-start.7
  229.7 4.6 copy-start.8
  242.7 3.7 copy-start.16
  242.7 4.1 copy-start.15
  242.7 41.4 %all-to-all-start.3 = ((bf16[8,128,768]{2,1,0:T(8,128)(2,1)}), bf16[8,128,768]{2,1,0:T(8,128)(2,1)S(1)}, u32[]{:S(2)}, u32[]{:S(2)}) async-start(bf16[8,128,768]{2,1,0:T(8,128)(2,1)} %bitcast.89), calls=%async_computation.3 | async-start | bytes 3145728 | tf_op jit(solution)/shard_map/all_to_all | solution.py:236
  284.4 1.7 copy-start.4
  284.8 1.8 copy-start.2
  437.2 5.4 copy-start.13
  437.2 93.2 %all-to-all-start.5 = ((bf16[8,33,6144]{2,1,0:T(8,128)(2,1)}), bf16[8,33,6144]{2,1,0:T(8,128)(2,1)}, u32[]{:S(2)}, u32[]{:S(2)}) async-start(bf16[8,33,6144]{2,1,0:T(8,128)(2,1)} %reshape.494), calls=%async_computation.5 | async-start | bytes 7864320 | tf_op jit(solution)/shard_map/all_to_all | solution.py:286
  543.8 2.1 copy-start.3
  543.8 2.3 copy-start.5
  546.1 2.3 copy-start.1
Sparse Core Ops, SparseCore 0:
  44.3 99.9 all-gather.4
  164.2 63.0 all-gather.2
where the time goes:
time: 560 us; the launch traced here: 556 us
  waiting for transfers between devices  275 us (49%)
  blocking collectives  91.9 us (16%)
  matrix products  66.4 us (12%)
  local copies, waits for them, and re-layouts  45.2 us (8%)
  starting transfers between devices  44 us (8%)
  other arithmetic  18.2 us (3%)
  between operations  14.6 us (3%)
    all_to_all x1, blocking collectives, per_device(): lax.all_to_all(send_rows, 'exp', split_axis=0, concat_axis=0, tiled=True)  91.9 us
    all_to_all x1, waiting for transfers between devices, per_device(): lax.all_to_all(expert_out.reshape(exp_count, CAP, piece_width), 'exp', sp...  87.3 us
    all_gather x1, waiting for transfers between devices, per_device(): shard_piece = lax.all_gather(attended, 'exp', axis=0, tiled=True)  63.2 us
    ppermute x8, waiting for transfers between devices, swapped(): lax.ppermute(x, axis, [(i, i ^ 1 << distance) for i in range(lax.axis_siz...  55.8 us
    all_to_all x1, waiting for transfers between devices, per_device(): lax.all_to_all(attn_block, 'exp', split_axis=0, concat_axis=1, tiled=True)  34.8 us
    ppermute x12, waiting for transfers between devices, passed_along(): return lax.ppermute(value, axis, pairs)  18.1 us
    dot_general x8, matrix products, per_device(): jnp.dot(rows_now, weight_slice, preferred_element_type=jnp.float32)  15.3 us
    ppermute x12, starting transfers between devices, passed_along(): return lax.ppermute(value, axis, pairs)  12.2 us
  transfers between devices with their start and end apart: 27, of which 18 were waited for; matrix products, arithmetic and copies ran while one was open for 6% of the time, Pallas kernels for 0%

commit v1 on v0

--- a/solution.py
+++ b/solution.py
@@ -233,7 +233,10 @@
     projected = carried
     projected = projected.reshape(block_len, column_count)
     attn_block = projected.astype(jnp.bfloat16)
-    attn_update = lax.all_to_all(attn_block, "exp", split_axis=0, concat_axis=1, tiled=True)
+    attn_update = jnp.concatenate(
+        lax.all_to_all(jnp.stack(jnp.split(attn_block, lax.axis_size("exp"), axis=0)), "exp", 0, 0),
+        axis=1,
+    )
     stream = residual.astype(jnp.float32) + attn_update.astype(jnp.float32)
     mean_sq = jnp.mean(stream * stream, axis=-1, keepdims=True)
     normed = (stream * lax.rsqrt(mean_sq + EPS) * norm_gain.astype(jnp.float32)).astype(

time: 560 us -> 574 us (1.025)
  local copies, waits for them, and re-layouts: 45.2 us -> 53.8 us
  other arithmetic: 18.2 us -> 24 us
where the time goes in v1:
time: 574 us; the launch traced here: 570 us
  waiting for transfers between devices  275 us (48%)
  blocking collectives  91.9 us (16%)
  matrix products  65.4 us (11%)
  local copies, waits for them, and re-layouts  53.8 us (9%)
  starting transfers between devices  44.6 us (8%)
  other arithmetic  24 us (4%)
  between operations  14.6 us (3%)
    all_to_all x1, blocking collectives, per_device(): lax.all_to_all(send_rows, 'exp', split_axis=0, concat_axis=0, tiled=True)  91.9 us
    all_to_all x1, waiting for transfers between devices, per_device(): lax.all_to_all(expert_out.reshape(exp_count, CAP, piece_width), 'exp', sp...  87.3 us
    all_gather x1, waiting for transfers between devices, per_device(): shard_piece = lax.all_gather(attended, 'exp', axis=0, tiled=True)  63.2 us
    ppermute x8, waiting for transfers between devices, swapped(): lax.ppermute(x, axis, [(i, i ^ 1 << distance) for i in range(lax.axis_siz...  55.8 us
    all_to_all x1, waiting for transfers between devices, per_device(): lax.all_to_all(jnp.stack(jnp.split(attn_block, lax.axis_size('exp'), axis...  34.8 us
    ppermute x12, waiting for transfers between devices, passed_along(): return lax.ppermute(value, axis, pairs)  18.1 us
    dot_general x8, matrix products, per_device(): jnp.dot(rows_now, weight_slice, preferred_element_type=jnp.float32)  14.4 us
    ppermute x12, starting transfers between devices, passed_along(): return lax.ppermute(value, axis, pairs)  12.2 us
  transfers between devices with their start and end apart: 27, of which 18 were waited for; matrix products, arithmetic and copies ran while one was open for 6% of the time, Pallas kernels for 0%

profile of v1, /device:TPU:0, one launch (start us, length us, event | category | flops | bytes accessed | tf_op | source)
XLA Modules:
  0.0 569.7 jit_solution(16537191967519510445)
XLA Ops:
  8.2 6.4 %all-to-all-start.1 = ((bf16[128,8,128]{2,0,1:T(8,128)(2,1)}), bf16[128,8,128]{2,0,1:T(8,128)(2,1)S(1)}, u32[]{:S(2)}, u32[]{:S(2)}) async-start(bf16[128,8,128]{2,0,1:T(8,128)(2,1)} %bitcast.3), calls=%async_computation.1 | async-start | bytes 524288 | tf_op jit(solution)/shard_map/all_to_all | solution.py:132
  15.5 8.8 %all-to-all-done.1 = bf16[128,8,128]{2,0,1:T(8,128)(2,1)S(1)} async-done(((bf16[128,8,128]{2,0,1:T(8,128)(2,1)}), bf16[128,8,128]{2,0,1:T(8,128)(2,1)S(1)}, u32[]{:S(2)}, u32[]{:S(2)}) %all-to-all-start.1) | async-done | bytes 262176 | tf_op jit(solution)/shard_map/all_to_all | solution.py:132
  25.0 3.4 all-to-all-start.2
  28.4 2.3 copy.183
  30.7 7.3 %all-to-all-done.2 = bf16[128,8,128]{2,0,1:T(8,128)(2,1)S(1)} async-done(((bf16[128,8,128]{2,0,1:T(8,128)(2,1)}), bf16[128,8,128]{2,0,1:T(8,128)(2,1)S(1)}, u32[]{:S(2)}, u32[]{:S(2)}) %all-to-all-start.2) | async-done | bytes 262176 | tf_op jit(solution)/shard_map/all_to_all | solution.py:133
  38.0 3.5 all-to-all-start
  44.1 4.0 collective-permute-done.2
  55.3 9.3 %collective-permute-done.5 = bf16[512,128]{1,0:T(8,128)(2,1)S(1)} collective-permute-done((bf16[512,128]{1,0:T(8,128)(2,1)S(1)}, bf16[512,128]{1,0:T(8,128)(2,1)S(1)}, u32[]{:S(2)}, u32[]{:S(2)}) %collective-permute-start.5) | collective-permute-done | bytes 131104 | tf_op jit(solution)/shard_map/ppermute | solution.py:19
  64.9 4.6 collective-permute-start.10
  69.5 2.7 collective-permute-done.7
  73.5 4.3 collective-permute-done.9
  79.4 3.6 collective-permute-done.10
  83.3 2.5 collective-permute-done.12
  86.1 2.5 collective-permute-done.11
  88.9 2.5 collective-permute-done.13
  97.1 11.4 %collective-permute-done = bf16[512,3,128]{2,0,1:T(8,128)(2,1)} collective-permute-done((bf16[512,3,128]{2,0,1:T(8,128)(2,1)}, bf16[512,3,128]{2,0,1:T(8,128)(2,1)}, u32[]{:S(2)}, u32[]{:S(2)}) %collective-permute-start) | collective-permute-done | bytes 393248 | tf_op jit(solution)/shard_map/ppermute | solution.py:19
  110.4 2.8 fusion.149
  113.3 15.1 %collective-permute-done.1 = bf16[512,3,128]{2,0,1:T(8,128)(2,1)S(1)} collective-permute-done((bf16[512,3,128]{2,0,1:T(8,128)(2,1)}, bf16[512,3,128]{2,0,1:T(8,128)(2,1)S(1)}, u32[]{:S(2)}, u32[]{:S(2)}) %collective-permute-start.1) | collective-permute-done | bytes 393248 | tf_op jit(solution)/shard_map/ppermute | solution.py:19
  147.0 7.8 %collective-permute-done.18 = bf16[512,384]{0,1:T(8,128)(2,1)S(1)} collective-permute-done((bf16[512,384]{0,1:T(8,128)(2,1)S(1)}, bf16[512,384]{0,1:T(8,128)(2,1)S(1)}, u32[]{:S(2)}, u32[]{:S(2)}) %collective-permute-start.18) | collective-permute-done | bytes 393248 | tf_op jit(solution)/shard_map/ppermute | solution.py:19
  155.7 7.4 %collective-permute-done.19 = bf16[512,384]{0,1:T(8,128)(2,1)S(1)} collective-permute-done((bf16[512,384]{0,1:T(8,128)(2,1)S(1)}, bf16[512,384]{0,1:T(8,128)(2,1)S(1)}, u32[]{:S(2)}, u32[]{:S(2)}) %collective-permute-start.19) | collective-permute-done | bytes 393248 | tf_op jit(solution)/shard_map/ppermute | solution.py:19
  164.1 63.2 %all-gather.3.cloned.1.call-done = bf16[8192,384]{0,1:T(8,128)(2,1)} async-done(((bf16[1024,384]{0,1:T(8,128)(2,1)}), bf16[8192,384]{0,1:T(8,128)(2,1)}) %all-gather.3.cloned.1.call-update) | async-done | bytes 6291472 | tf_op jit(solution)/shard_map/all_gather | solution.py:219
  227.3 2.5 fusion.167
  229.8 2.5 fusion.169
  232.2 2.1 fusion.171
  238.9 2.8 add_convert_fusion
  247.2 4.3 all-to-all-start.3
  254.5 34.8 %all-to-all-done.3 = bf16[8,128,768]{2,1,0:T(8,128)(2,1)} async-done(((bf16[8,128,768]{2,1,0:T(8,128)(2,1)}), bf16[8,128,768]{2,1,0:T(8,128)(2,1)}, u32[]{:S(2)}, u32[]{:S(2)}) %all-to-all-start.3) | async-done | bytes 1572896 | tf_op jit(solution)/shard_map/all_to_all | solution.py:237
  291.0 2.3 copy.210
  293.4 2.4 copy.211
  295.8 3.1 multiply_reduce_fusion
  298.9 2.4 multiply_convert_fusion
  301.3 5.0 gather_fusion
  306.3 4.9 gather.13
  311.3 2.5 select_multiply_fusion
  313.8 91.9 %all_to_all.60 = bf16[8,33,6144]{2,1,0:T(8,128)(2,1)} all-to-all(bf16[8,33,6144]{2,1,0:T(8,128)(2,1)S(1)} %select_multiply_fusion), channel_id=1, replica_groups=mesh['seq'=4,'exp'=8] {'exp'}, dimensions={0} | all-to-all | bytes 6488064 | tf_op jit(solution)/shard_map/all_to_all | solution.py:270
  405.7 5.0 reshape.492
  410.7 9.1 %fusion.80 = bf16[264,1024]{1,0:T(8,128)(2,1)S(1)} fusion(bf16[264,6144]{1,0:T(8,128)(2,1)} %reshape.492, bf16[1,6144,1024]{2,1,0:T(8,128)(2,1)} %param.20), kind=kOutput, calls=%fused_computation.117 | convolution fusion | flops 3322159104 | bytes 16367616 | tf_op jit(solution)/shard_map/dot_general | solution.py:272
  419.8 9.1 %fusion.6 = f32[264,8192]{1,0:T(8,128)} fusion(bf16[1,2,512,8192]{3,2,1,0:T(8,128)(2,1)} %param.21, bf16[264,1024]{1,0:T(8,128)(2,1)S(1)} %fusion.80), kind=kOutput, calls=%fused_computation.9 | convolution fusion | flops 2214592512 | bytes 17309696 | tf_op jit(solution)/shard_map/dot_general | solution.py:278
  428.9 11.2 %fusion.158 = bf16[264,512]{1,0:T(8,128)(2,1)S(1)} fusion(bf16[1,8192,512]{2,1,0:T(8,128)(2,1)} %param.22, f32[264,8192]{1,0:T(8,128)} %fusion.6, bf16[1,2,512,8192]{3,2,1,0:T(8,128)(2,1)} %param.21, bf16[264,1024]{1,0:T(8,128)(2,1)S(1)} %fusion.80), kind=kOutput, calls=%fused_computation.143 | convolution fusion | flops 4442296320 | bytes 25968640 | tf_op jit(solution)/shard_map/dot_general | solution.py:281
  440.1 6.4 %convolution_convert_fusion = bf16[264,6144]{1,0:T(8,128)(2,1)} fusion(bf16[264,512]{1,0:T(8,128)(2,1)S(1)} %fusion.158, bf16[1,512,6144]{2,1,0:T(8,128)(2,1)} %param.23), kind=kOutput, calls=%fused_computation.13 | convolution fusion | flops 1662566400 | bytes 9805824 | tf_op jit(solution)/shard_map/dot_general | solution.py:286
  446.4 4.9 reshape.493
  451.4 4.9 all-to-all-start.5
  457.3 87.3 %all-to-all-done.5 = bf16[8,33,6144]{2,1,0:T(8,128)(2,1)} async-done(((bf16[8,33,6144]{2,1,0:T(8,128)(2,1)}), bf16[8,33,6144]{2,1,0:T(8,128)(2,1)}, u32[]{:S(2)}, u32[]{:S(2)}) %all-to-all-start.5) | async-done | bytes 3244064 | tf_op jit(solution)/shard_map/all_to_all | solution.py:289
  544.6 3.3 reshape.494
  547.9 4.1 gather_fusion.1
  552.0 5.9 %gather.15 = bf16[128,2,6144]{2,1,0:T(2,128)(2,1)S(1)} reshape(bf16[256,6144]{1,0:T(8,128)(2,1)} %gather_fusion.1) | data formatting | bytes 6291456 | tf_op jit(solution)/shard_map/jit(_take)/gather | solution.py:301
  557.9 2.0 fusion.19
  560.3 2.3 fusion.17
  (190 shorter events, 60.5 us)
Async XLA Ops:
  6.5 0.9 copy-start
  8.2 16.1 %all-to-all-start.1 = ((bf16[128,8,128]{2,0,1:T(8,128)(2,1)}), bf16[128,8,128]{2,0,1:T(8,128)(2,1)S(1)}, u32[]{:S(2)}, u32[]{:S(2)}) async-start(bf16[128,8,128]{2,0,1:T(8,128)(2,1)} %bitcast.3), calls=%async_computation.1 | async-start | bytes 524288 | tf_op jit(solution)/shard_map/all_to_all | solution.py:132
  25.0 13.1 %all-to-all-start.2 = ((bf16[128,8,128]{2,0,1:T(8,128)(2,1)}), bf16[128,8,128]{2,0,1:T(8,128)(2,1)S(1)}, u32[]{:S(2)}, u32[]{:S(2)}) async-start(bf16[128,8,128]{2,0,1:T(8,128)(2,1)} %bitcast.8), calls=%async_computation.2 | async-start | bytes 524288 | tf_op jit(solution)/shard_map/all_to_all | solution.py:133
  38.0 53.9 %all-to-all-start = ((bf16[128,8,384]{0,2,1:T(8,128)(2,1)}), bf16[128,8,384]{0,2,1:T(8,128)(2,1)S(1)}, u32[]{:S(2)}, u32[]{:S(2)}) async-start(bf16[128,8,384]{0,2,1:T(8,128)(2,1)} %bitcast), calls=%async_computation | async-start | bytes 1572864 | tf_op jit(solution)/shard_map/all_to_all | solution.py:131
  41.6 122.5 %all-gather.5.cloned.1.call-start = ((), (), s32[]{:S(2)}) async-start(), calls=%async_computation.7 | async-start | bytes 5898240 | tf_op jit(solution)/shard_map/all_gather | solution.py:215
  41.7 6.4 %collective-permute-start.2 = (bf16[512,128]{1,0:T(8,128)(2,1)S(1)}, bf16[512,128]{1,0:T(8,128)(2,1)S(1)}, u32[]{:S(2)}, u32[]{:S(2)}) collective-permute-start(bf16[512,128]{1,0:T(8,128)(2,1)S(1)} %bitcast.434), channel_id=1, source_target_pairs={{0,8},{8,0},{16,24},{24,16},{1,9},{9,1},{17,25},{25,17},{2,10},{10... | collective-permute-start | bytes 393224 | tf_op jit(solution)/shard_map/ppermute | solution.py:19
  43.3 26.2 %copy-start.9 = (bf16[4,128,1,128]{3,1,0,2:T(8,128)(2,1)}, bf16[4,128,1,128]{3,1,0,2:T(8,128)(2,1)S(1)}, u32[]{:S(2)}) copy-start(bf16[4,128,1,128]{3,1,0,2:T(8,128)(2,1)S(1)} %get-tuple-element.29) | copy-start | bytes 393220
  43.3 7.0 %collective-permute-start.4 = (bf16[512,128]{1,0:T(8,128)(2,1)S(1)}, bf16[512,128]{1,0:T(8,128)(2,1)S(1)}, u32[]{:S(2)}, u32[]{:S(2)}) collective-permute-start(bf16[512,128]{1,0:T(8,128)(2,1)S(1)} %bitcast.435), channel_id=1, source_target_pairs={{0,8},{8,0},{16,24},{24,16},{1,9},{9,1},{17,25},{25,17},{2,10},{10... | collective-permute-start | bytes 393224 | tf_op jit(solution)/shard_map/ppermute | solution.py:19
  43.9 183.4 %all-gather.3.cloned.1.call-start = ((), (), s32[]{:S(2)}) async-start(), calls=%async_computation.6 | async-start | bytes 7077888 | tf_op jit(solution)/shard_map/all_gather | solution.py:219
  48.1 5.7 %collective-permute-start.3 = (bf16[512,128]{1,0:T(8,128)(2,1)S(1)}, bf16[512,128]{1,0:T(8,128)(2,1)S(1)}, u32[]{:S(2)}, u32[]{:S(2)}) collective-permute-start(bf16[512,128]{1,0:T(8,128)(2,1)S(1)} %collective-permute-done.2), channel_id=1, source_target_pairs={{0,16},{8,24},{16,0},{24,8},{1,17},{9,25},{17,1},{25,9},{2,18},{10... | collective-permute-start | bytes 393224 | tf_op jit(solution)/shard_map/ppermute | solution.py:19
  50.3 14.3 %collective-permute-start.5 = (bf16[512,128]{1,0:T(8,128)(2,1)S(1)}, bf16[512,128]{1,0:T(8,128)(2,1)S(1)}, u32[]{:S(2)}, u32[]{:S(2)}) collective-permute-start(bf16[512,128]{1,0:T(8,128)(2,1)S(1)} %collective-permute-done.4), channel_id=1, source_target_pairs={{0,16},{8,24},{16,0},{24,8},{1,17},{9,25},{17,1},{25,9},{2,18},{10... | collective-permute-start | bytes 393224 | tf_op jit(solution)/shard_map/ppermute | solution.py:19
  51.8 13.0 %collective-permute-start.6 = (bf16[512,128]{1,0:T(8,128)(2,1)S(1)}, bf16[512,128]{1,0:T(8,128)(2,1)S(1)}, u32[]{:S(2)}, u32[]{:S(2)}) collective-permute-start(bf16[512,128]{1,0:T(8,128)(2,1)S(1)} %bitcast.426), channel_id=1, source_target_pairs={{0,8},{8,16},{16,24},{24,0},{1,9},{9,17},{17,25},{25,1},{2,10},{10... | collective-permute-start | bytes 393224 | tf_op jit(solution)/shard_map/ppermute | solution.py:25
  53.3 16.1 %collective-permute-start.8 = (bf16[512,128]{1,0:T(8,128)(2,1)S(1)}, bf16[512,128]{1,0:T(8,128)(2,1)S(1)}, u32[]{:S(2)}, u32[]{:S(2)}) collective-permute-start(bf16[512,128]{1,0:T(8,128)(2,1)S(1)} %bitcast.431), channel_id=1, source_target_pairs={{0,8},{8,16},{16,24},{24,0},{1,9},{9,17},{17,25},{25,1},{2,10},{10... | collective-permute-start | bytes 393224 | tf_op jit(solution)/shard_map/ppermute | solution.py:25
  53.8 18.4 %collective-permute-start.7 = (bf16[512,128]{1,0:T(8,128)(2,1)S(1)}, bf16[512,128]{1,0:T(8,128)(2,1)S(1)}, u32[]{:S(2)}, u32[]{:S(2)}) collective-permute-start(bf16[512,128]{1,0:T(8,128)(2,1)S(1)} %collective-permute-done.3), channel_id=1, source_target_pairs={{0,8},{8,16},{16,24},{24,0},{1,9},{9,17},{17,25},{25,1},{2,10},{10... | collective-permute-start | bytes 393224 | tf_op jit(solution)/shard_map/ppermute | solution.py:25
  64.6 21.5 %copy-start.11 = (bf16[512,128]{1,0:T(8,128)(2,1)}, bf16[512,128]{1,0:T(8,128)(2,1)S(1)}, u32[]{:S(2)}) copy-start(bf16[512,128]{1,0:T(8,128)(2,1)S(1)} %collective-permute-done.5) | copy-start | bytes 393220
  64.6 13.2 %collective-permute-start.9 = (bf16[512,128]{1,0:T(8,128)(2,1)S(1)}, bf16[512,128]{1,0:T(8,128)(2,1)S(1)}, u32[]{:S(2)}, u32[]{:S(2)}) collective-permute-start(bf16[512,128]{1,0:T(8,128)(2,1)S(1)} %collective-permute-done.5), channel_id=1, source_target_pairs={{0,8},{8,16},{16,24},{24,0},{1,9},{9,17},{17,25},{25,1},{2,10},{10... | collective-permute-start | bytes 393224 | tf_op jit(solution)/shard_map/ppermute | solution.py:25
  64.9 18.1 %collective-permute-start.10 = (bf16[512,128]{1,0:T(8,128)(2,1)S(1)}, bf16[512,128]{1,0:T(8,128)(2,1)S(1)}, u32[]{:S(2)}, u32[]{:S(2)}) collective-permute-start(bf16[512,128]{1,0:T(8,128)(2,1)S(1)} %collective-permute-done.6), channel_id=1, source_target_pairs={{0,8},{8,16},{16,24},{24,0},{1,9},{9,17},{17,25},{25,1},{2,10},{10... | collective-permute-start | bytes 393224 | tf_op jit(solution)/shard_map/ppermute | solution.py:25
  69.4 16.4 %collective-permute-start.12 = (bf16[512,128]{1,0:T(8,128)(2,1)S(1)}, bf16[512,128]{1,0:T(8,128)(2,1)S(1)}, u32[]{:S(2)}, u32[]{:S(2)}) collective-permute-start(bf16[512,128]{1,0:T(8,128)(2,1)S(1)} %collective-permute-done.8), channel_id=1, source_target_pairs={{0,8},{8,16},{16,24},{24,0},{1,9},{9,17},{17,25},{25,1},{2,10},{10... | collective-permute-start | bytes 393224 | tf_op jit(solution)/shard_map/ppermute | solution.py:25
  72.2 16.4 %collective-permute-start.11 = (bf16[512,128]{1,0:T(8,128)(2,1)S(1)}, bf16[512,128]{1,0:T(8,128)(2,1)S(1)}, u32[]{:S(2)}, u32[]{:S(2)}) collective-permute-start(bf16[512,128]{1,0:T(8,128)(2,1)S(1)} %collective-permute-done.7), channel_id=1, source_target_pairs={{0,8},{8,16},{16,24},{24,0},{1,9},{9,17},{17,25},{25,1},{2,10},{10... | collective-permute-start | bytes 393224 | tf_op jit(solution)/shard_map/ppermute | solution.py:25
  77.8 13.6 %collective-permute-start.13 = (bf16[512,128]{1,0:T(8,128)(2,1)S(1)}, bf16[512,128]{1,0:T(8,128)(2,1)S(1)}, u32[]{:S(2)}, u32[]{:S(2)}) collective-permute-start(bf16[512,128]{1,0:T(8,128)(2,1)S(1)} %collective-permute-done.9), channel_id=1, source_target_pairs={{0,8},{8,16},{16,24},{24,0},{1,9},{9,17},{17,25},{25,1},{2,10},{10... | collective-permute-start | bytes 393224 | tf_op jit(solution)/shard_map/ppermute | solution.py:25
  83.0 57.6 %collective-permute-start.14 = (bf16[512,128]{1,0:T(8,128)(2,1)S(1)}, bf16[512,128]{1,0:T(8,128)(2,1)S(1)}, u32[]{:S(2)}, u32[]{:S(2)}) collective-permute-start(bf16[512,128]{1,0:T(8,128)(2,1)S(1)} %collective-permute-done.10), channel_id=1, source_target_pairs={{0,8},{8,16},{16,24},{24,0},{1,9},{9,17},{17,25},{25,1},{2,10},{10... | collective-permute-start | bytes 393224 | tf_op jit(solution)/shard_map/ppermute | solution.py:25
  85.8 56.3 %collective-permute-start.16 = (bf16[512,128]{1,0:T(8,128)(2,1)S(1)}, bf16[512,128]{1,0:T(8,128)(2,1)S(1)}, u32[]{:S(2)}, u32[]{:S(2)}) collective-permute-start(bf16[512,128]{1,0:T(8,128)(2,1)S(1)} %collective-permute-done.12), channel_id=1, source_target_pairs={{0,8},{8,16},{16,24},{24,0},{1,9},{9,17},{17,25},{25,1},{2,10},{10... | collective-permute-start | bytes 393224 | tf_op jit(solution)/shard_map/ppermute | solution.py:25
  88.6 52.0 %collective-permute-start.15 = (bf16[512,128]{1,0:T(8,128)(2,1)S(1)}, bf16[512,128]{1,0:T(8,128)(2,1)S(1)}, u32[]{:S(2)}, u32[]{:S(2)}) collective-permute-start(bf16[512,128]{1,0:T(8,128)(2,1)S(1)} %collective-permute-done.11), channel_id=1, source_target_pairs={{0,8},{8,16},{16,24},{24,0},{1,9},{9,17},{17,25},{25,1},{2,10},{10... | collective-permute-start | bytes 393224 | tf_op jit(solution)/shard_map/ppermute | solution.py:25
  91.4 50.7 %collective-permute-start.17 = (bf16[512,128]{1,0:T(8,128)(2,1)S(1)}, bf16[512,128]{1,0:T(8,128)(2,1)S(1)}, u32[]{:S(2)}, u32[]{:S(2)}) collective-permute-start(bf16[512,128]{1,0:T(8,128)(2,1)S(1)} %collective-permute-done.13), channel_id=1, source_target_pairs={{0,8},{8,16},{16,24},{24,0},{1,9},{9,17},{17,25},{25,1},{2,10},{10... | collective-permute-start | bytes 393224 | tf_op jit(solution)/shard_map/ppermute | solution.py:25
  93.4 15.2 %collective-permute-start = (bf16[512,3,128]{2,0,1:T(8,128)(2,1)}, bf16[512,3,128]{2,0,1:T(8,128)(2,1)}, u32[]{:S(2)}, u32[]{:S(2)}) collective-permute-start(bf16[512,3,128]{2,0,1:T(8,128)(2,1)} %copy.191), channel_id=1, source_target_pairs={{0,8},{8,0},{16,24},{24,16},{1,9},{9,1},{17,25},{25,17},{2,10},{10... | collective-permute-start | bytes 1179656 | tf_op jit(solution)/shard_map/ppermute | solution.py:19
  95.5 1.6 copy-start.6
  96.2 12.3 %copy-start.14 = (f32[512,3]{0,1:T(4,128)}, f32[512,3]{0,1:T(4,128)S(1)}, u32[]{:S(2)}) copy-start(f32[512,3]{0,1:T(4,128)S(1)} %get-tuple-element.47) | copy-start | bytes 18436
  108.5 19.9 %collective-permute-start.1 = (bf16[512,3,128]{2,0,1:T(8,128)(2,1)}, bf16[512,3,128]{2,0,1:T(8,128)(2,1)S(1)}, u32[]{:S(2)}, u32[]{:S(2)}) collective-permute-start(bf16[512,3,128]{2,0,1:T(8,128)(2,1)} %collective-permute-done), channel_id=1, source_target_pairs={{0,16},{8,24},{16,0},{24,8},{1,17},{9,25},{17,1},{25,9},{2,18},{10... | collective-permute-start | bytes 1179656 | tf_op jit(solution)/shard_map/ppermute | solution.py:19
  129.8 1.3 copy-start.12
  131.1 1.1 copy-start.10
  145.7 9.1 %collective-permute-start.18 = (bf16[512,384]{0,1:T(8,128)(2,1)S(1)}, bf16[512,384]{0,1:T(8,128)(2,1)S(1)}, u32[]{:S(2)}, u32[]{:S(2)}) collective-permute-start(bf16[512,384]{0,1:T(8,128)(2,1)S(1)} %fusion.181), channel_id=1, source_target_pairs={{0,8},{8,0},{16,24},{24,16},{1,9},{9,1},{17,25},{25,17},{2,10},{10... | collective-permute-start | bytes 1179656 | tf_op jit(solution)/shard_map/ppermute | solution.py:19
  154.8 8.2 %collective-permute-start.19 = (bf16[512,384]{0,1:T(8,128)(2,1)S(1)}, bf16[512,384]{0,1:T(8,128)(2,1)S(1)}, u32[]{:S(2)}, u32[]{:S(2)}) collective-permute-start(bf16[512,384]{0,1:T(8,128)(2,1)S(1)} %collective-permute-done.18), channel_id=1, source_target_pairs={{0,16},{8,24},{16,0},{24,8},{1,17},{9,25},{17,1},{25,9},{2,18},{10... | collective-permute-start | bytes 1179656 | tf_op jit(solution)/shard_map/ppermute | solution.py:19
  227.3 5.0 copy-start.7
  229.7 4.6 copy-start.8
  241.7 9.8 %copy-start.16 = (s32[128,2]{0,1:T(2,128)S(1)}, s32[128,2]{0,1:T(2,128)}, u32[]{:S(2)}) copy-start(s32[128,2]{0,1:T(2,128)} %param.19) | copy-start | bytes 3076
  242.4 9.5 %copy-start.15 = (bf16[6144]{0:T(1024)(128)(2,1)S(1)}, bf16[6144]{0:T(1024)(128)(2,1)}, u32[]{:S(2)}) copy-start(bf16[6144]{0:T(1024)(128)(2,1)} %param.17) | copy-start | bytes 36868
  247.2 42.1 %all-to-all-start.3 = ((bf16[8,128,768]{2,1,0:T(8,128)(2,1)}), bf16[8,128,768]{2,1,0:T(8,128)(2,1)}, u32[]{:S(2)}, u32[]{:S(2)}) async-start(bf16[8,128,768]{2,1,0:T(8,128)(2,1)} %fusion.223), calls=%async_computation.3 | async-start | bytes 3145728 | tf_op jit(solution)/shard_map/all_to_all | solution.py:237
  295.8 3.1 copy-start.2
  295.8 3.1 copy-start.4
  451.4 5.4 copy-start.13
  451.4 93.2 %all-to-all-start.5 = ((bf16[8,33,6144]{2,1,0:T(8,128)(2,1)}), bf16[8,33,6144]{2,1,0:T(8,128)(2,1)}, u32[]{:S(2)}, u32[]{:S(2)}) async-start(bf16[8,33,6144]{2,1,0:T(8,128)(2,1)} %reshape.493), calls=%async_computation.5 | async-start | bytes 7864320 | tf_op jit(solution)/shard_map/all_to_all | solution.py:289
  557.9 2.1 copy-start.3
  557.9 2.3 copy-start.5
  560.3 2.3 copy-start.1
Sparse Core Ops, SparseCore 0:
  44.3 99.9 all-gather.4
  164.2 63.0 all-gather.2
